TPU v7x, 32 devices: a whole 2x2x4 slice. The times are simulated.
32 devices in a mesh: gx: 4 (over y, x), gy: 2 (over core), gz: 4 (over z).
Axes of the slice: x: 2, y: 2, z: 4, core: 2. Of those that a mesh axis runs over, the one named last changes fastest.
Arguments:
- right_side: float32 [64, 64, 512], P('gx', 'gy', 'gz'), may hold values from -8 to 8
- diagonal: float32 [64, 64, 512], P('gx', 'gy', 'gz'), may hold values from 0.16 to 6.1
Outputs:
- solution_field: float32 [64, 64, 512], P('gx', 'gy', 'gz')
- residual: float32 [64, 64, 512], P('gx', 'gy', 'gz')
All inputs are finite; a program needn't handle non-finite values.
Results may differ from a plain program's by a relative error of at most 0.0003.
Values sent between devices are 32-bit elements; how exact they have to be, the bound alone decides.
A program may use at most 128 MiB of HBM per device.

v0:
```python
import functools

import jax
import jax.numpy as jnp
from jax import lax
from jax.experimental import pallas as pl
from jax.experimental.pallas import tpu as pltpu
from jax.sharding import PartitionSpec as P

ITERS = 2
LANES = 128
H = 8
MESH = pl.DeviceIdType.MESH
F32, BF16 = jnp.float32, jnp.bfloat16
UF, UR, U1, UC, UM, UP = 4, 4, 4, 8, 4, 4
OFFSETS = [
    (a, b, c) for a in (-1, 0, 1) for b in (-1, 0, 1) for c in (-1, 0, 1) if (a, b, c) != (0, 0, 0)
]
OFFSETS.sort(key=lambda o: (o[0] == 0, o[2] == 0, o[1] == 0))


def cheb_terms(lower):
    upper = 58.0
    theta = (upper + lower) / 2.0
    delta = (upper - lower) / 2.0
    return theta, delta, theta / delta


def cheb_two(lower):
    theta, delta, sigma = cheb_terms(lower)
    rho = 1.0 / sigma
    rho_next = 1.0 / (2.0 * sigma - rho)
    gain = 2.0 * rho_next / delta
    k2 = gain / theta
    k3 = (1.0 + rho_next * rho) / theta + gain - 27.0 * k2
    return k2, k3


def halves(v):
    high = v.astype(BF16)
    return high, (v - high.astype(F32)).astype(BF16)


def ml(m, v):
    return lax.dot(m[...], jnp.concatenate(halves(v), axis=0), preferred_element_type=F32)


def mr(v, m):
    high, low = halves(v)
    return lax.dot(high, m[...], preferred_element_type=F32) + lax.dot(
        low, m[...], preferred_element_type=F32
    )


def iota(shape, dim):
    return lax.broadcasted_iota(jnp.int32, shape, dim)


def ring(s, rows, lanes):
    s = s + pltpu.roll(s, 1, 0) + pltpu.roll(s, rows - 1, 0)
    return s + pltpu.roll(s, 1, 1) + pltpu.roll(s, lanes - 1, 1)


def box(ref, p):
    s = ref[p - 1] + ref[p] + ref[p + 1]
    return ring(s, *s.shape)


def kernel(
    dims, x_ref, d_ref, sol_ref, res_ref,
    land, edge, face, D, R, Z, T, W, S0,
    land1, edge1, face1, D1, R1a, R1, Z1, T1, send1,
    slots, tile, rows, row, G, E, Y, Q, M0, M1, LyR, RzR, LyP, RzP, LyR2, RzR2, LyP2, RzP2,
    ssem, rsem, gssem, grsem,
):
    GX, GY, GZ = dims
    N = GX * GY * GZ
    nx, ny, nz = x_ref.shape
    n1x, n1y, n1z = nx // 2, ny // 2, nz // 2
    n2x, n2y, n2z = nx // 4, ny // 4, nz // 4
    Y0, Y1 = ny + 2 * H, n1y + 2 * H
    NX2, NY2, NZ2 = GX * n2x, GY * n2y, GZ * n2z
    ix, iy, iz = lax.axis_index("gx"), lax.axis_index("gy"), lax.axis_index("gz")
    me = (ix * GY + iy) * GZ + iz
    k2, k3 = cheb_two(7.0)
    W0 = 2 * LANES

    WIDE = (H, 6, 6)

    def cut(o, n, h):
        if o == 0:
            return 0, H, n
        if o > 0:
            return n - h, H - h, h
        return 0, H + n, h

    def there(o, sign):
        ok = None
        for i, g, d in ((ix, GX, o[0]), (iy, GY, o[1]), (iz, GZ, o[2])):
            d = d * sign
            if d:
                t = (i + d >= 0) & (i + d < g)
                ok = t if ok is None else ok & t
        return ok

    def copy(ex, k, core, faces, dst, dst_edge, sizes, hx):
        a, b, c = OFFSETS[k]
        xs, xd, xn = cut(a, sizes[0], hx)
        ys, yd, yn = cut(b, sizes[1], H)
        if c == 0:
            src = core.at[pl.ds(xs, xn), pl.ds(ys, yn)]
            to = dst.at[pl.ds(xd, xn), pl.ds(yd, yn)]
        else:
            f, side = (1, 0) if c > 0 else (0, 1)
            src = faces(f).at[pl.ds(ys, yn)]
            to = dst_edge.at[side, 1 - a, pl.ds(yd, yn)]
        return pltpu.make_async_remote_copy(
            src_ref=src, dst_ref=to, send_sem=ssem.at[ex, k], recv_sem=rsem.at[ex, k],
            device_id={"gx": ix + a, "gy": iy + b, "gz": iz + c}, device_id_type=MESH,
        )

    def args0(e, core):
        return (core, lambda f: face.at[e, f], land.at[e], edge.at[e], (nx, ny, nz), WIDE[e])

    def args1(e):
        return (send1.at[e], lambda f: face1.at[e], land1.at[e], edge1.at[e], (n1x, n1y, n1z), 5)

    def start(exs, packed=(True, False)):
        for k, o in enumerate(OFFSETS):
            if (o[2] != 0) not in packed:
                continue

            @pl.when(there(o, 1))
            def _():
                for ex, args in exs:
                    copy(ex, k, *args).start()

    def finish(exs):
        for k, o in enumerate(OFFSETS):
            @pl.when(there(o, -1))
            def _():
                for ex, args in exs:
                    copy(ex, k, *args).wait_recv()

            @pl.when(there(o, 1))
            def _():
                for ex, args in exs:
                    copy(ex, k, *args).wait_send()

    def gather_copy(k, send_slot, sender, target):
        return pltpu.make_async_remote_copy(
            src_ref=tile.at[k] if k < 3 else row.at[k - 3],
            dst_ref=slots.at[k, sender] if k < 3 else rows.at[k - 3, sender],
            send_sem=gssem.at[k, send_slot], recv_sem=grsem.at[k, sender],
            device_id={
                "gx": target // (GY * GZ), "gy": (target // GZ) % GY, "gz": target % GZ,
            },
            device_id_type=MESH,
        )

    def gather_start(k):
        def body(d, _):
            gather_copy(k, d, me, (me + d) % N).start()
            return 0
        lax.fori_loop(1, N, body, 0)
        if k < 3:
            slots[k, me] = tile[k]
        else:
            rows[k - 3, me] = row[k - 3]

    def gather_finish(k):
        def body(d, _):
            s = (me + N - d) % N
            gather_copy(k, d, s, s).wait_recv()
            gather_copy(k, d, s, s).wait_send()
            return 0
        lax.fori_loop(1, N, body, 0)

    lane = iota((1, LANES), 1)

    def pack0(e, core):
        first = jnp.zeros((ny, LANES), F32)
        last = jnp.zeros((ny, LANES), F32)
        for x in range(nx):
            v = core[x]
            here = (lane >= H * x) & (lane < H * x + H)
            first = jnp.where(here, pltpu.roll(v, H * x, 1) if x else v, first)
            last = jnp.where(here, pltpu.roll(v, (H * x + H) % LANES, 1) if (H * x + H) % LANES else v, last)
        face[e, 0] = first
        face[e, 1] = last

    both = [(0, args0(0, d_ref)), (1, args0(1, x_ref))]
    start(both, (False,))
    pack0(0, d_ref)
    pack0(1, x_ref)
    start(both, (True,))

    def off0(l):
        return jnp.where(l < 192, l, l - 256)

    def off1(l):
        return jnp.where(l < 96, l, l - 128)

    def pair(fine, coarse):
        return (fine == 2 * coarse) | (fine == 2 * coarse + 1)

    def inside(v, i, n, g):
        v = v + i * n
        return (v >= 0) & (v < g * n)

    def f(cond, value=1.0):
        return jnp.where(cond, F32(value), F32(0.0))

    def twice(m):
        return jnp.concatenate([m, m], axis=1).astype(BF16)

    def near0(z):
        return (z >= -H) & (z < nz + H)

    def near1(z):
        return (z >= -H) & (z < n1z + H)

    yy, zz = iota((Y0, W0), 0) - H, off0(iota((Y0, W0), 1))
    M0[...] = f(inside(yy, iy, ny, GY) & inside(zz, iz, nz, GZ) & near0(zz))
    yy, zz = iota((Y1, LANES), 0) - H, off1(iota((Y1, LANES), 1))
    M1[...] = f(inside(yy, iy, n1y, GY) & inside(zz, iz, n1z, GZ) & near1(zz))
    c, v = iota((Y1, Y0), 0) - H, iota((Y1, Y0), 1) - H
    LyR[...] = twice(f(pair(v, c) & inside(c, iy, n1y, GY), 0.5))
    v, c = iota((Y0, Y1), 0) - H, iota((Y0, Y1), 1) - H
    LyP[...] = twice(f(pair(v, c) & inside(c, iy, n1y, GY)))
    v, c = off0(iota((W0, LANES), 0)), off1(iota((W0, LANES), 1))
    RzR[...] = f(pair(v, c) & inside(c, iz, n1z, GZ) & near0(v)).astype(BF16)
    c, v = off1(iota((LANES, W0), 0)), off0(iota((LANES, W0), 1))
    RzP[...] = f(pair(v, c) & inside(c, iz, n1z, GZ) & near0(v)).astype(BF16)
    c, v = iota((n2y, Y1), 0), iota((n2y, Y1), 1) - H
    LyR2[...] = twice(f(pair(v, c), 0.5))
    v, c = off1(iota((LANES, LANES), 0)), iota((LANES, LANES), 1) % n2z
    RzR2[...] = f(pair(v, c)).astype(BF16)
    v, c = iota((Y1, NY2), 0) - H + iy * n1y, iota((Y1, NY2), 1)
    LyP2[...] = twice(f(pair(v, c)))
    c, v = iota((NZ2, LANES), 0), off1(iota((NZ2, LANES), 1))
    RzP2[...] = f(pair(v + iz * n1z, c) & near1(v)).astype(BF16)

    def xin0(p):
        return f(inside(p - H, ix, nx, GX))

    def xin1(p):
        return f(inside(p - H, ix, n1x, GX))

    def loop(lo, hi, body, group=1):
        count = hi - lo
        while count % group:
            group -= 1

        def step(i, _):
            stores = [body(lo + i * group + k) for k in range(group)]
            for store in stores:
                store()
            return 0
        lax.fori_loop(0, count // group, step, 0)

    def put(ref, p, v):
        def store():
            ref[p] = v
        return store

    def merged0(e, core, p, b, sx):
        right = pltpu.roll(edge[e, 1, b], (LANES - H * sx) % LANES, 1)
        left = pltpu.roll(edge[e, 0, b], (2 * LANES - H - H * sx) % LANES, 1)
        return land[e, p], jnp.where(lane < H, right, left)

    def merge0(e, core, emit):
        land[e, H : H + nx, H : H + ny] = core[...]
        for b, lo, hi, shift in (
            (0, H - WIDE[e], H, nx - H), (1, H, H + nx, -H), (2, H + nx, H + nx + WIDE[e], -H - nx)
        ):
            def body(p, b=b, shift=shift):
                t0, t1 = merged0(e, core, p, b, p + shift)
                ok = M0[...] * xin0(p) > 0.5
                return emit(p, jnp.where(ok, jnp.concatenate([t0, t1], axis=1), 0.0))
            loop(lo, hi, body, UM)

    finish([(0, args0(0, d_ref)), (1, args0(1, x_ref))])

    merge0(0, d_ref, lambda p, v: put(D, p, v))
    merge0(1, x_ref, lambda p, v: put(R, p, v))

    def make_d1(p):
        s = D[2 * p - H] + D[2 * p - H + 1]
        return put(D1, p, 0.25 * mr(ml(LyR, s), RzR))

    loop(4, n1x + 2 * H - 4, make_d1, UR)

    def coarsen(k, scale, plane):
        total = jnp.zeros((n2y, LANES), F32)
        for x in range(n2x):
            s = plane(H + 2 * x) + plane(H + 2 * x + 1)
            v = mr(ml(LyR2, s), RzR2)
            total = total + jnp.where((lane >= n2z * x) & (lane < n2z * x + n2z), v, 0.0)
        tile[k] = total * scale

    coarsen(0, 0.25, lambda p: D1[p])
    gather_start(0)

    def spread(k, dst):
        def body(a):
            for x in range(n2x):
                for b in range(GY):
                    for t in range(NZ2 // LANES):
                        v = jnp.zeros((n2y, LANES), F32)
                        per = LANES // n2z
                        for q in range(per):
                            src = slots[k, (a * GY + b) * GZ + t * per + q]
                            shift = (n2z * (q - x)) % LANES
                            src = pltpu.roll(src, shift, 1) if shift else src
                            v = jnp.where((lane >= n2z * q) & (lane < n2z * q + n2z), src, v)
                        dst[a * n2x + x + 2, n2y * b : n2y * b + n2y, LANES * t : LANES * t + LANES] = v
            return lambda: None
        loop(0, GX, body)

    rows2, lanes2 = iota((NY2, NZ2), 0), iota((NY2, NZ2), 1)

    def box2(ref, p):
        s = ref[p - 1] + ref[p] + ref[p + 1]
        s = (
            s
            + jnp.where(rows2 > 0, pltpu.roll(s, 1, 0), 0.0)
            + jnp.where(rows2 < NY2 - 1, pltpu.roll(s, NY2 - 1, 0), 0.0)
        )
        return (
            s
            + jnp.where(lanes2 > 0, pltpu.roll(s, 1, 1), 0.0)
            + jnp.where(lanes2 < NZ2 - 1, pltpu.roll(s, NZ2 - 1, 1), 0.0)
        )

    zero2 = jnp.zeros((2, NY2, NZ2), F32)
    for ref in (G, Q, Y):
        ref[0:2] = zero2
        ref[NX2 + 2 : NX2 + 4] = zero2

    def coarse():
        theta, delta, sigma = cheb_terms(1.0)
        rho1 = 1.0 / sigma
        rho2 = 1.0 / (2.0 * sigma - rho1)
        rho3 = 1.0 / (2.0 * sigma - rho2)
        a2, b2 = rho2 * rho1, 2.0 * rho2 / delta
        a3, b3 = rho3 * rho2, 2.0 * rho3 / delta

        def first(p):
            g = G[p]
            remain = g - ((27.0 + E[p]) * g - box2(G, p)) * (1.0 / theta)
            a, b = put(Q, p, (a2 / theta) * g + b2 * remain), put(Y, p, remain)
            return lambda: (a(), b())

        def second(p):
            q, g = Q[p], G[p]
            remain = Y[p] - ((27.0 + E[p]) * q - box2(Q, p))
            return put(Y, p, (1.0 / theta) * g + (1.0 + a3) * q + b3 * remain)

        def third(p):
            y = Y[p]
            left = G[p] - ((27.0 + E[p]) * y - box2(Y, p))
            shift = jnp.sum(left, axis=1, keepdims=True) / jnp.sum(1.0 + E[p], axis=1, keepdims=True)
            return put(Q, p, y + shift)

        for body in (first, second, third):
            loop(2, NX2 + 2, body, UC)

    def smooth1(ref, p):
        return ref[p] * (k3 - k2 * D1[p]) + k2 * box(ref, p)

    def precondition(it):
        ex = 2 + it

        def down0(p):
            return put(Z, p, (M0[...] * xin0(p)) * (R[p] * (k3 - k2 * D[p]) + k2 * box(R, p)))

        loop(H - 5, H + nx + 5, down0, UF)

        def rest0(p):
            return R[p] - ((27.0 + D[p]) * Z[p] - box(Z, p))

        def down1(p):
            s = rest0(2 * p - H) + rest0(2 * p - H + 1)
            return put(R1a, p, xin1(p) * mr(ml(LyR, s), RzR))

        loop(H - 2, H + n1x + 2, down1, UR)

        edges = jnp.zeros((n1y, LANES), F32)
        for x in range(n1x):
            v = R1a[H + x, H : H + n1y]
            send1[it, x] = v
            lo = 2 * H * x
            low = pltpu.roll(v, lo, 1) if lo else v
            up = pltpu.roll(v, (lo + 2 * H - n1z) % LANES, 1) if (lo + 2 * H - n1z) % LANES else v
            edges = jnp.where((lane >= lo) & (lane < lo + H), low, edges)
            edges = jnp.where((lane >= lo + H) & (lane < lo + 2 * H), up, edges)
        face1[it] = edges
        start([(ex, args1(it))])

        def z1a(p):
            return put(Z1, p, (M1[...] * xin1(p)) * smooth1(R1a, p))

        loop(H - 1, H + n1x + 1, z1a, U1)
        coarsen(1 + it, 1.0, lambda p: R1a[p] - ((27.0 + D1[p]) * Z1[p] - box(Z1, p)))
        gather_start(1 + it)

        finish([(ex, args1(it))])

        land1[it, H : H + n1x, H : H + n1y] = send1[it]
        for b, lo, hi, shift in (
            (0, H - 5, H, n1x - H), (1, H, H + n1x, -H), (2, H + n1x, H + n1x + 5, -H - n1x)
        ):
            def body(p, b=b, shift=shift):
                sx = p + shift
                right = pltpu.roll(edge1[it, 1, b], (LANES + n1z - 2 * H * sx) % LANES, 1)
                left = pltpu.roll(edge1[it, 0, b], (2 * LANES - 2 * H - 2 * H * sx) % LANES, 1)
                v = jnp.where(lane < n1z, land1[it, p], jnp.where(lane < n1z + H, right, left))
                return put(R1, p, jnp.where(M1[...] * xin1(p) > 0.5, v, 0.0))
            loop(lo, hi, body, 5)

        def z1b(p):
            return put(Z1, p, (M1[...] * xin1(p)) * smooth1(R1, p))

        loop(H - 4, H + n1x + 4, z1b, U1)

        if it == 0:
            gather_finish(0)
            spread(0, E)
        gather_finish(1 + it)
        spread(1 + it, G)
        coarse()

        def up1(q):
            v = mr(ml(LyP2, Q[ix * n2x + q]), RzP2)
            p = H - 4 + 2 * q
            a, b = put(Z1, p, Z1[p] + v), put(Z1, p + 1, Z1[p + 1] + v)
            return lambda: (a(), b())

        loop(0, n2x + 4, up1, 4)

        def t1(p):
            return put(T1, p, (M1[...] * xin1(p)) * (R1[p] - ((27.0 + D1[p]) * Z1[p] - box(Z1, p))))

        loop(H - 3, H + n1x + 3, t1, U1)

        def z1c(p):
            return put(Z1, p, Z1[p] + (M1[...] * xin1(p)) * smooth1(T1, p))

        loop(H - 2, H + n1x + 2, z1c, U1)

        def up0(p):
            v = mr(ml(LyP, Z1[p]), RzP)
            q = 2 * p - H
            a, b = put(Z, q, Z[q] + v), put(Z, q + 1, Z[q + 1] + v)
            return lambda: (a(), b())

        loop(H - 2, H + n1x + 2, up0, UR)

        def t0(p):
            return put(T, p, (M0[...] * xin0(p)) * rest0(p))

        loop(H - 2, H + nx + 2, t0, UF)

        def z0(p):
            return put(Z, p, Z[p] + (M0[...] * xin0(p)) * (T[p] * (k3 - k2 * D[p]) + k2 * box(T, p)))

        loop(H - 1, H + nx + 1, z0, UF)

    core = (slice(H, H + ny), slice(0, nz))

    def products(it):
        def one(x, carry):
            p = x + H
            z = Z[p]
            w = ((27.0 + D[p]) * z - box(Z, p))[core[0], core[1]]
            z = z[core[0], core[1]]
            W[it, x] = w
            S0[it, x] = z
            r = R[p, core[0], core[1]]
            out = [carry[0] + r * z, carry[1] + z * w]
            if it:
                out.append(carry[2] + z * W[0, x])
            return tuple(out)

        def body(i, carry):
            for k in range(UP):
                carry = one(i * UP + k, carry)
            return carry

        init = tuple(jnp.zeros((ny, nz), F32) for _ in range(3 if it else 2))
        sums = lax.fori_loop(0, nx // UP, body, init)
        v = jnp.zeros((1, LANES), F32)
        for i, s in enumerate(sums):
            s = jnp.sum(jnp.sum(s, axis=0, keepdims=True), axis=1, keepdims=True)
            v = jnp.where(lane == i, s, v)
        row[it] = v
        gather_start(3 + it)

    def total(k):
        gather_finish(k)

        def body(n, acc):
            return acc + rows[k - 3, n]

        acc = lax.fori_loop(0, N, body, jnp.zeros((1, LANES), F32))
        return acc[:, 0:1], acc[:, 1:2], acc[:, 2:3]

    precondition(0)
    products(0)
    image = args0(2, W.at[0])
    start([(4, image)], (False,))
    pack0(2, W.at[0])
    start([(4, image)], (True,))
    rz0, curve0, _ = total(3)
    alpha0 = rz0 / curve0
    finish([(4, image)])

    def put_image(p, v):
        return put(R, p, R[p] - alpha0 * v)

    merge0(2, W.at[0], put_image)
    precondition(1)
    products(1)
    rz1, zw, zq = total(4)
    beta = rz1 / rz0
    curve = zw + 2.0 * beta * zq + beta * beta * curve0
    alpha = rz1 / curve

    def last(x):
        z = S0[0, x]
        sol_ref[x] = alpha0 * z + alpha * (S0[1, x] + beta * z)
        res_ref[x] = R[x + H, core[0], core[1]] - alpha * (W[1, x] + beta * W[0, x])
        return lambda: None

    loop(0, nx, last, 4)


def solution(mesh):
    dims = (mesh.shape["gx"], mesh.shape["gy"], mesh.shape["gz"])
    N = dims[0] * dims[1] * dims[2]

    def local(right_side, diagonal):
        nx, ny, nz = right_side.shape
        assert nz == LANES and nx * H == LANES and (nx // 4) * (nz // 4) == LANES and ny == 32
        n1x, n1y, n2y = nx // 2, ny // 2, ny // 4
        X0, Y0, X1, Y1 = nx + 2 * H, ny + 2 * H, n1x + 2 * H, n1y + 2 * H
        NX2, NY2, NZ2 = dims[0] * nx // 4, dims[1] * n2y, dims[2] * nz // 4
        W0 = 2 * LANES
        vm = lambda *s: pltpu.VMEM(s, F32)
        vb = lambda *s: pltpu.VMEM(s, BF16)
        dma = pltpu.SemaphoreType.DMA
        scratch = [
            vm(3, X0, Y0, LANES), vm(3, 2, 3, Y0, LANES), vm(3, 2, ny, LANES),
            vm(X0, Y0, W0), vm(X0, Y0, W0), vm(X0, Y0, W0), vm(X0, Y0, W0),
            vm(2, nx, ny, nz), vm(2, nx, ny, nz),
            vm(2, X1, Y1, LANES), vm(2, 2, 3, Y1, LANES), vm(2, n1y, LANES),
            vm(X1, Y1, LANES), vm(X1, Y1, LANES), vm(X1, Y1, LANES), vm(X1, Y1, LANES), vm(X1, Y1, LANES),
            vm(2, n1x, n1y, LANES),
            vm(3, N, 8, LANES), vm(3, 8, LANES), vm(2, N, 1, LANES), vm(2, 1, LANES),
            vm(NX2 + 4, NY2, NZ2), vm(NX2 + 4, NY2, NZ2), vm(NX2 + 4, NY2, NZ2), vm(NX2 + 4, NY2, NZ2),
            vm(Y0, W0), vm(Y1, LANES),
            vb(Y1, 2 * Y0), vb(W0, LANES), vb(Y0, 2 * Y1), vb(LANES, W0),
            vb(n2y, 2 * Y1), vb(LANES, LANES), vb(Y1, 2 * NY2), vb(NZ2, LANES),
            dma((5, 26)), dma((5, 26)), dma((5, N)), dma((5, N)),
        ]
        shape = jax.ShapeDtypeStruct(right_side.shape, F32)
        return pl.pallas_call(
            functools.partial(kernel, dims),
            out_shape=(shape, shape),
            in_specs=[pl.BlockSpec(memory_space=pltpu.VMEM)] * 2,
            out_specs=[pl.BlockSpec(memory_space=pltpu.VMEM)] * 2,
            scratch_shapes=scratch,
            compiler_params=pltpu.CompilerParams(has_side_effects=True),
        )(right_side, diagonal)

    placed = (P("gx", "gy", "gz"), P("gx", "gy", "gz"))
    return jax.shard_map(local, mesh=mesh, in_specs=placed, out_specs=placed, check_vma=False)
```

profile of v0, /device:TPU:0, one launch (start us, length us, event | category | flops | bytes accessed | tf_op | source)
XLA Modules:
  0.0 96.8 jit_solution(8499725385596751721)
XLA Ops:
  0.6 93.7 %shard_map.41 = (f32[16,32,128]{2,1,0:T(8,128)}, f32[16,32,128]{2,1,0:T(8,128)}) custom-call(f32[16,32,128]{2,1,0:T(8,128)} %x_ref.1, f32[16,32,128]{2,1,0:T(8,128)} %d_ref.1), custom_call_target="tpu_custom_call" | custom-call | tf_op jit(solution)/shard_map/pallas_call | solution.py:568
  94.3 0.0 copy-start
  94.3 1.7 %copy.6 = f32[16,32,128]{2,1,0:T(8,128)} copy(f32[16,32,128]{2,1,0:T(8,128)} %get-tuple-element.4) | data formatting | bytes 524288
  96.1 0.0 copy-done
  96.1 0.7 copy.7
Async XLA Ops:
  94.3 1.7 %copy-start = (f32[16,32,128]{2,1,0:T(8,128)S(1)}, f32[16,32,128]{2,1,0:T(8,128)}, u32[]{:S(2)}) copy-start(f32[16,32,128]{2,1,0:T(8,128)} %get-tuple-element.5) | copy-start | bytes 786436
where the time goes:
time: 96.9 us; the launch traced here: 96.8 us
  Pallas kernels  93.7 us (97%)
  local copies, waits for them, and re-layouts  2.42 us (2%)
    pallas_call x1, Pallas kernels, local(): pl.pallas_call(functools.partial(kernel, dims), out_shape=(shape, shape),...  93.7 us
    unnamed x4, local copies, waits for them, and re-layouts  2.42 us

commit v1 on v0

--- a/solution.py
+++ b/solution.py
@@ -67,11 +67,12 @@
 
 
 def kernel(
-    dims, x_ref, d_ref, sol_ref, res_ref,
-    land, edge, face, D, R, Z, T, W, S0,
+    dims, x_hbm, d_hbm, sol_ref, res_ref,
+    x_ref, d_ref, land, edge, face, corner, cland, D, R, Z, T, W, S0,
     land1, edge1, face1, D1, R1a, R1, Z1, T1, send1,
-    slots, tile, rows, row, G, E, Y, Q, M0, M1, LyR, RzR, LyP, RzP, LyR2, RzR2, LyP2, RzP2,
-    ssem, rsem, gssem, grsem,
+    slots, tile, eslots, etile, rows, row, G, E, Y, Q, M0, M1,
+    LyR, RzR, LyP, RzP, LyR2, RzR2, LyP2, RzP2,
+    ssem, rsem, gssem, grsem, csem,
 ):
     GX, GY, GZ = dims
     N = GX * GY * GZ
@@ -85,7 +86,26 @@
     k2, k3 = cheb_two(7.0)
     W0 = 2 * LANES
 
-    WIDE = (H, 6, 6)
+    FAR = (3, 4, 4)
+    NEAR = 2
+    DEEP = LANES // ny
+
+    def device(n):
+        return {"gx": n // (GY * GZ), "gy": (n // GZ) % GY, "gz": n % GZ}
+
+    loads = [
+        pltpu.make_async_copy(src, dst, csem.at[i])
+        for i, (src, dst) in enumerate(((d_hbm, d_ref), (x_hbm, x_ref)))
+    ]
+    barrier = pltpu.get_barrier_semaphore()
+
+    def greet(d, _):
+        pl.semaphore_signal(barrier, inc=1, device_id=device((me + d) % N), device_id_type=MESH)
+        return 0
+
+    lax.fori_loop(1, N, greet, 0)
+    for load in loads:
+        load.start()
 
     def cut(o, n, h):
         if o == 0:
@@ -103,59 +123,89 @@
                 ok = t if ok is None else ok & t
         return ok
 
-    def copy(ex, k, core, faces, dst, dst_edge, sizes, hx):
-        a, b, c = OFFSETS[k]
-        xs, xd, xn = cut(a, sizes[0], hx)
-        ys, yd, yn = cut(b, sizes[1], H)
-        if c == 0:
-            src = core.at[pl.ds(xs, xn), pl.ds(ys, yn)]
-            to = dst.at[pl.ds(xd, xn), pl.ds(yd, yn)]
-        else:
-            f, side = (1, 0) if c > 0 else (0, 1)
-            src = faces(f).at[pl.ds(ys, yn)]
-            to = dst_edge.at[side, 1 - a, pl.ds(yd, yn)]
+    def remote(ex, slot, o, src, dst):
         return pltpu.make_async_remote_copy(
-            src_ref=src, dst_ref=to, send_sem=ssem.at[ex, k], recv_sem=rsem.at[ex, k],
-            device_id={"gx": ix + a, "gy": iy + b, "gz": iz + c}, device_id_type=MESH,
+            src_ref=src, dst_ref=dst, send_sem=ssem.at[ex, slot], recv_sem=rsem.at[ex, slot],
+            device_id={"gx": ix + o[0], "gy": iy + o[1], "gz": iz + o[2]}, device_id_type=MESH,
         )
 
-    def args0(e, core):
-        return (core, lambda f: face.at[e, f], land.at[e], edge.at[e], (nx, ny, nz), WIDE[e])
-
-    def args1(e):
-        return (send1.at[e], lambda f: face1.at[e], land1.at[e], edge1.at[e], (n1x, n1y, n1z), 5)
-
-    def start(exs, packed=(True, False)):
-        for k, o in enumerate(OFFSETS):
-            if (o[2] != 0) not in packed:
-                continue
-
-            @pl.when(there(o, 1))
+    def fine(e, core):
+        def make(k, far):
+            o = a, b, c = OFFSETS[k]
+            ys, yd, yn = cut(b, ny, H)
+            slot = k
+            if c == 0:
+                if a == 0:
+                    xs, xd, xn = 0, H, nx
+                else:
+                    lo, hi = (NEAR, FAR[e]) if far else (0, NEAR)
+                    xs, xd, xn = (nx - hi, H - hi, hi - lo) if a > 0 else (lo, H + nx + lo, hi - lo)
+                    slot = k + far * len(OFFSETS)
+                src = core.at[pl.ds(xs, xn), pl.ds(ys, yn)]
+                dst = land.at[e, pl.ds(xd, xn), pl.ds(yd, yn)]
+            else:
+                f, side = (1, 0) if c > 0 else (0, 1)
+                if a == 0:
+                    src, dst = face.at[e, f, pl.ds(ys, yn)], edge.at[e, side, 1, pl.ds(yd, yn)]
+                else:
+                    src, dst = corner.at[e, (1 - a) // 2, f], cland.at[e, side, (1 - a) // 2, 1 - b]
+            return remote(e, slot, o, src, dst)
+        return make
+
+    def level1(ex, e, h):
+        def make(k, far):
+            o = a, b, c = OFFSETS[k]
+            xs, xd, xn = cut(a, n1x, h)
+            ys, yd, yn = cut(b, n1y, H)
+            if c == 0:
+                src = send1.at[e, pl.ds(xs, xn), pl.ds(ys, yn)]
+                dst = land1.at[e, pl.ds(xd, xn), pl.ds(yd, yn)]
+            else:
+                src, dst = face1.at[e, pl.ds(ys, yn)], edge1.at[e, 0 if c > 0 else 1, 1 - a, pl.ds(yd, yn)]
+            return remote(ex, k, o, src, dst)
+        return make
+
+    FLAT = [k for k, o in enumerate(OFFSETS) if o[2] == 0]
+    PACKED = [k for k, o in enumerate(OFFSETS) if o[2] != 0]
+    WIDER = [k for k, o in enumerate(OFFSETS) if o[2] == 0 and o[0] != 0]
+    sent = []
+
+    def start(makers, ks, far=0):
+        for k in ks:
+            @pl.when(there(OFFSETS[k], 1))
             def _():
-                for ex, args in exs:
-                    copy(ex, k, *args).start()
-
-    def finish(exs):
-        for k, o in enumerate(OFFSETS):
-            @pl.when(there(o, -1))
+                for make in makers:
+                    make(k, far).start()
+        sent.append((makers, ks, far))
+
+    def finish(makers, ks, far=0):
+        for k in ks:
+            @pl.when(there(OFFSETS[k], -1))
             def _():
-                for ex, args in exs:
-                    copy(ex, k, *args).wait_recv()
-
-            @pl.when(there(o, 1))
-            def _():
-                for ex, args in exs:
-                    copy(ex, k, *args).wait_send()
+                for make in makers:
+                    make(k, far).wait_recv()
+
+    def drain():
+        for makers, ks, far in sent:
+            for k in ks:
+                @pl.when(there(OFFSETS[k], 1))
+                def _():
+                    for make in makers:
+                        make(k, far).wait_send()
+
+    def ends(k, sender):
+        if k == 0:
+            return etile, eslots.at[sender]
+        if k < 3:
+            return tile.at[k - 1], slots.at[k - 1, sender]
+        return row.at[k - 3], rows.at[k - 3, sender]
 
     def gather_copy(k, send_slot, sender, target):
+        src, dst = ends(k, sender)
         return pltpu.make_async_remote_copy(
-            src_ref=tile.at[k] if k < 3 else row.at[k - 3],
-            dst_ref=slots.at[k, sender] if k < 3 else rows.at[k - 3, sender],
+            src_ref=src, dst_ref=dst,
             send_sem=gssem.at[k, send_slot], recv_sem=grsem.at[k, sender],
-            device_id={
-                "gx": target // (GY * GZ), "gy": (target // GZ) % GY, "gz": target % GZ,
-            },
-            device_id_type=MESH,
+            device_id=device(target), device_id_type=MESH,
         )
 
     def gather_start(k):
@@ -163,16 +213,19 @@
             gather_copy(k, d, me, (me + d) % N).start()
             return 0
         lax.fori_loop(1, N, body, 0)
-        if k < 3:
-            slots[k, me] = tile[k]
-        else:
-            rows[k - 3, me] = row[k - 3]
+        src, dst = ends(k, me)
+        dst[...] = src[...]
 
     def gather_finish(k):
         def body(d, _):
             s = (me + N - d) % N
             gather_copy(k, d, s, s).wait_recv()
-            gather_copy(k, d, s, s).wait_send()
+            return 0
+        lax.fori_loop(1, N, body, 0)
+
+    def gather_drain(k):
+        def body(d, _):
+            gather_copy(k, d, me, me).wait_send()
             return 0
         lax.fori_loop(1, N, body, 0)
 
@@ -186,14 +239,35 @@
             here = (lane >= H * x) & (lane < H * x + H)
             first = jnp.where(here, pltpu.roll(v, H * x, 1) if x else v, first)
             last = jnp.where(here, pltpu.roll(v, (H * x + H) % LANES, 1) if (H * x + H) % LANES else v, last)
-        face[e, 0] = first
-        face[e, 1] = last
-
-    both = [(0, args0(0, d_ref)), (1, args0(1, x_ref))]
-    start(both, (False,))
+        for f, v in enumerate((first, last)):
+            face[e, f] = v
+            for i, base in enumerate((nx - DEEP, 0)):
+                fold = jnp.zeros((H, LANES), F32)
+                for k in range(ny // H):
+                    lo = H * DEEP * k
+                    shift = (lo - H * base) % LANES
+                    part = v[H * k : H * k + H]
+                    part = pltpu.roll(part, shift, 1) if shift else part
+                    fold = jnp.where((lane >= lo) & (lane < lo + H * DEEP), part, fold)
+                corner[e, i, f] = fold
+
+    def unfold(e):
+        for side in range(2):
+            for i in range(2):
+                for k in range(-1, ny // H + 1):
+                    v = cland[e, side, i, 0 if k < 0 else 2 if k == ny // H else 1]
+                    shift = -H * DEEP * (k % (ny // H)) % LANES
+                    edge[e, side, 2 * i, H * k + H : H * k + 2 * H] = pltpu.roll(v, shift, 1) if shift else v
+
+    pl.semaphore_wait(barrier, N - 1)
+    for load in loads:
+        load.wait()
+    both = [fine(0, d_ref), fine(1, x_ref)]
+    start(both, FLAT)
     pack0(0, d_ref)
     pack0(1, x_ref)
-    start(both, (True,))
+    start(both, PACKED)
+    start(both, WIDER, 1)
 
     def off0(l):
         return jnp.where(l < 192, l, l - 256)
@@ -257,7 +331,10 @@
             for store in stores:
                 store()
             return 0
-        lax.fori_loop(0, count // group, step, 0)
+        if count == group:
+            step(0, 0)
+        else:
+            lax.fori_loop(0, count // group, step, 0)
 
     def put(ref, p, v):
         def store():
@@ -269,54 +346,123 @@
         left = pltpu.roll(edge[e, 0, b], (2 * LANES - H - H * sx) % LANES, 1)
         return land[e, p], jnp.where(lane < H, right, left)
 
-    def merge0(e, core, emit):
-        land[e, H : H + nx, H : H + ny] = core[...]
-        for b, lo, hi, shift in (
-            (0, H - WIDE[e], H, nx - H), (1, H, H + nx, -H), (2, H + nx, H + nx + WIDE[e], -H - nx)
-        ):
+    def merge0(e, core, emit, far=False):
+        near = ((0, H - NEAR, H, DEEP - H), (1, H, H + nx, -H), (2, H + nx, H + nx + NEAR, -H - nx))
+        rest = ((0, H - FAR[e], H - NEAR, DEEP - H), (2, H + nx + NEAR, H + nx + FAR[e], -H - nx))
+        if not far:
+            unfold(e)
+            land[e, H : H + nx, H : H + ny] = core[...]
+        for b, lo, hi, shift in rest if far else near:
             def body(p, b=b, shift=shift):
                 t0, t1 = merged0(e, core, p, b, p + shift)
                 ok = M0[...] * xin0(p) > 0.5
                 return emit(p, jnp.where(ok, jnp.concatenate([t0, t1], axis=1), 0.0))
             loop(lo, hi, body, UM)
 
-    finish([(0, args0(0, d_ref)), (1, args0(1, x_ref))])
-
-    merge0(0, d_ref, lambda p, v: put(D, p, v))
-    merge0(1, x_ref, lambda p, v: put(R, p, v))
+    none = jnp.zeros((2, Y1, LANES), F32)
+    R1a[H - 2 : H] = none
+    R1a[H + n1x : H + n1x + 2] = none
+
+    def put_d(p, v):
+        return put(D, p, v)
+
+    def put_r(p, v):
+        return put(R, p, v)
+
+    finish(both, FLAT)
+    finish(both, PACKED)
+    merge0(0, d_ref, put_d)
+    merge0(1, x_ref, put_r)
 
     def make_d1(p):
         s = D[2 * p - H] + D[2 * p - H + 1]
         return put(D1, p, 0.25 * mr(ml(LyR, s), RzR))
 
-    loop(4, n1x + 2 * H - 4, make_d1, UR)
-
-    def coarsen(k, scale, plane):
+    loop(H - 1, H + n1x + 1, make_d1, 5)
+
+    def pack1(e, src):
+        edges = jnp.zeros((n1y, LANES), F32)
+        for x in range(n1x):
+            v = src[H + x, H : H + n1y]
+            send1[e, x] = v
+            lo = 2 * H * x
+            low = pltpu.roll(v, lo, 1) if lo else v
+            up = pltpu.roll(v, (lo + 2 * H - n1z) % LANES, 1) if (lo + 2 * H - n1z) % LANES else v
+            edges = jnp.where((lane >= lo) & (lane < lo + H), low, edges)
+            edges = jnp.where((lane >= lo + H) & (lane < lo + 2 * H), up, edges)
+        face1[e] = edges
+
+    def merge1(e, h, dst, inner=True):
+        land1[e, H : H + n1x, H : H + n1y] = send1[e]
+        for b, lo, hi, shift in (
+            (0, H - h, H, n1x - H), (1, H, H + n1x, -H), (2, H + n1x, H + n1x + h, -H - n1x)
+        ):
+            if b == 1 and not inner:
+                continue
+
+            def body(p, b=b, shift=shift):
+                sx = p + shift
+                right = pltpu.roll(edge1[e, 1, b], (LANES + n1z - 2 * H * sx) % LANES, 1)
+                left = pltpu.roll(edge1[e, 0, b], (2 * LANES - 2 * H - 2 * H * sx) % LANES, 1)
+                v = jnp.where(lane < n1z, land1[e, p], jnp.where(lane < n1z + H, right, left))
+                return put(dst, p, jnp.where(M1[...] * xin1(p) > 0.5, v, 0.0))
+            loop(lo, hi, body, 5)
+
+    pack1(2, D1)
+    start([level1(3, 2, 4)], FLAT + PACKED)
+
+    def coarse_tile(s):
+        return mr(ml(LyR2, s), RzR2)
+
+    def coarsen(plane):
         total = jnp.zeros((n2y, LANES), F32)
         for x in range(n2x):
-            s = plane(H + 2 * x) + plane(H + 2 * x + 1)
-            v = mr(ml(LyR2, s), RzR2)
+            v = coarse_tile(plane(H + 2 * x) + plane(H + 2 * x + 1))
             total = total + jnp.where((lane >= n2z * x) & (lane < n2z * x + n2z), v, 0.0)
-        tile[k] = total * scale
-
-    coarsen(0, 0.25, lambda p: D1[p])
+        return total
+
+    etile[...] = coarsen(lambda p: D1[p]) * 0.25
     gather_start(0)
 
-    def spread(k, dst):
+    def block(src, q, at):
+        shift = (n2z * (q - at)) % LANES
+        return pltpu.roll(src, shift, 1) if shift else src
+
+    def along(load, at):
+        v = None
+        for q in range(LANES // n2z):
+            part = block(load(q), q, at)
+            v = part if v is None else jnp.where(lane >= n2z * q, part, v)
+        return v
+
+    PER = LANES // n2z
+
+    def spread(load, dst, ring):
         def body(a):
             for x in range(n2x):
                 for b in range(GY):
                     for t in range(NZ2 // LANES):
-                        v = jnp.zeros((n2y, LANES), F32)
-                        per = LANES // n2z
-                        for q in range(per):
-                            src = slots[k, (a * GY + b) * GZ + t * per + q]
-                            shift = (n2z * (q - x)) % LANES
-                            src = pltpu.roll(src, shift, 1) if shift else src
-                            v = jnp.where((lane >= n2z * q) & (lane < n2z * q + n2z), src, v)
+                        v = along(lambda q: load((a * GY + b) * GZ + t * PER + q, 0), x)
                         dst[a * n2x + x + 2, n2y * b : n2y * b + n2y, LANES * t : LANES * t + LANES] = v
             return lambda: None
         loop(0, GX, body)
+        if not ring:
+            return
+
+        def edges(a):
+            for b in range(GY):
+                for t in range(NZ2 // LANES):
+                    for i, p in ((0, a * n2x + 1), (1, (a + 1) * n2x + 2)):
+                        v = jnp.concatenate([
+                            along(lambda q: load((a * GY + b) * GZ + t * PER + q, 1), i + h) for h in (0, 2)
+                        ], axis=0)
+                        at = (p, slice(n2y * b, n2y * b + n2y), slice(LANES * t, LANES * t + LANES))
+                        dst[at] = dst[at] + v
+            return lambda: None
+        loop(0, GX, edges)
+        zero = jnp.zeros((NY2, NZ2), F32)
+        dst[1] = zero
+        dst[NX2 + 2] = zero
 
     rows2, lanes2 = iota((NY2, NZ2), 0), iota((NY2, NZ2), 1)
 
@@ -370,54 +516,54 @@
         return ref[p] * (k3 - k2 * D1[p]) + k2 * box(ref, p)
 
     def precondition(it):
-        ex = 2 + it
+        ex = 4 + it
 
         def down0(p):
             return put(Z, p, (M0[...] * xin0(p)) * (R[p] * (k3 - k2 * D[p]) + k2 * box(R, p)))
 
-        loop(H - 5, H + nx + 5, down0, UF)
+        loop(H - 1, H + nx + 1, down0, 6)
 
         def rest0(p):
             return R[p] - ((27.0 + D[p]) * Z[p] - box(Z, p))
 
         def down1(p):
             s = rest0(2 * p - H) + rest0(2 * p - H + 1)
-            return put(R1a, p, xin1(p) * mr(ml(LyR, s), RzR))
-
-        loop(H - 2, H + n1x + 2, down1, UR)
-
-        edges = jnp.zeros((n1y, LANES), F32)
-        for x in range(n1x):
-            v = R1a[H + x, H : H + n1y]
-            send1[it, x] = v
-            lo = 2 * H * x
-            low = pltpu.roll(v, lo, 1) if lo else v
-            up = pltpu.roll(v, (lo + 2 * H - n1z) % LANES, 1) if (lo + 2 * H - n1z) % LANES else v
-            edges = jnp.where((lane >= lo) & (lane < lo + H), low, edges)
-            edges = jnp.where((lane >= lo + H) & (lane < lo + 2 * H), up, edges)
-        face1[it] = edges
-        start([(ex, args1(it))])
+            return put(R1a, p, mr(ml(LyR, s), RzR))
+
+        loop(H, H + n1x, down1, UR)
+
+        pack1(it, R1a)
+        fine1 = [level1(ex, it, 5)]
+        start(fine1, FLAT + PACKED)
+
+        Z1[H - 3 : H - 1] = none
+        Z1[H + n1x + 1 : H + n1x + 3] = none
 
         def z1a(p):
             return put(Z1, p, (M1[...] * xin1(p)) * smooth1(R1a, p))
 
-        loop(H - 1, H + n1x + 1, z1a, U1)
-        coarsen(1 + it, 1.0, lambda p: R1a[p] - ((27.0 + D1[p]) * Z1[p] - box(Z1, p)))
+        loop(H - 1, H + n1x + 1, z1a, 5)
+
+        def rest1(p):
+            return R1a[p] - ((27.0 + D1[p]) * Z1[p] - box(Z1, p))
+
+        tile[it, 0:n2y] = coarsen(rest1)
+        low = coarse_tile(box(Z1, H - 2) + rest1(H - 1))
+        high = coarse_tile(rest1(H + n1x) + box(Z1, H + n1x + 1))
+        low, high = (jnp.where(lane < 2 * n2z, v, pltpu.roll(v, n2y // 2, 0)) for v in (low, high))
+        ring2 = jnp.where(lane // n2z % 2 == 0, low, high)
+        tile[it, n2y : n2y + n2y // 2] = ring2[0 : n2y // 2]
         gather_start(1 + it)
 
-        finish([(ex, args1(it))])
-
-        land1[it, H : H + n1x, H : H + n1y] = send1[it]
-        for b, lo, hi, shift in (
-            (0, H - 5, H, n1x - H), (1, H, H + n1x, -H), (2, H + n1x, H + n1x + 5, -H - n1x)
-        ):
-            def body(p, b=b, shift=shift):
-                sx = p + shift
-                right = pltpu.roll(edge1[it, 1, b], (LANES + n1z - 2 * H * sx) % LANES, 1)
-                left = pltpu.roll(edge1[it, 0, b], (2 * LANES - 2 * H - 2 * H * sx) % LANES, 1)
-                v = jnp.where(lane < n1z, land1[it, p], jnp.where(lane < n1z + H, right, left))
-                return put(R1, p, jnp.where(M1[...] * xin1(p) > 0.5, v, 0.0))
-            loop(lo, hi, body, 5)
+        far(it)
+        for lo, hi in ((H - 3, H - 1), (H + nx + 1, H + nx + 3)):
+            loop(lo, hi, down0, 2)
+
+        finish(fine1, FLAT + PACKED)
+        merge1(it, 5, R1)
+        if it == 0:
+            finish([level1(3, 2, 4)], FLAT + PACKED)
+            merge1(2, 4, D1, False)
 
         def z1b(p):
             return put(Z1, p, (M1[...] * xin1(p)) * smooth1(R1, p))
@@ -426,9 +572,9 @@
 
         if it == 0:
             gather_finish(0)
-            spread(0, E)
+            spread(lambda n, r: eslots[n], E, False)
         gather_finish(1 + it)
-        spread(1 + it, G)
+        spread(lambda n, r: slots[it, n, n2y:] if r else slots[it, n, 0:n2y], G, True)
         coarse()
 
         def up1(q):
@@ -506,15 +652,26 @@
         acc = lax.fori_loop(0, N, body, jnp.zeros((1, LANES), F32))
         return acc[:, 0:1], acc[:, 1:2], acc[:, 2:3]
 
+    def far(it):
+        if it == 0:
+            finish(both, WIDER, 1)
+            merge0(0, d_ref, put_d, True)
+            merge0(1, x_ref, put_r, True)
+        else:
+            finish(image, WIDER, 1)
+            merge0(2, W.at[0], put_image, True)
+
     precondition(0)
     products(0)
-    image = args0(2, W.at[0])
-    start([(4, image)], (False,))
+    image = [fine(2, W.at[0])]
+    start(image, FLAT)
     pack0(2, W.at[0])
-    start([(4, image)], (True,))
+    start(image, PACKED)
+    start(image, WIDER, 1)
     rz0, curve0, _ = total(3)
     alpha0 = rz0 / curve0
-    finish([(4, image)])
+    finish(image, FLAT)
+    finish(image, PACKED)
 
     def put_image(p, v):
         return put(R, p, R[p] - alpha0 * v)
@@ -534,6 +691,9 @@
         return lambda: None
 
     loop(0, nx, last, 4)
+    drain()
+    for k in range(5):
+        gather_drain(k)
 
 
 def solution(mesh):
@@ -551,27 +711,29 @@
         vb = lambda *s: pltpu.VMEM(s, BF16)
         dma = pltpu.SemaphoreType.DMA
         scratch = [
+            vm(nx, ny, nz), vm(nx, ny, nz),
             vm(3, X0, Y0, LANES), vm(3, 2, 3, Y0, LANES), vm(3, 2, ny, LANES),
+            vm(3, 2, 2, H, LANES), vm(3, 2, 2, 3, H, LANES),
             vm(X0, Y0, W0), vm(X0, Y0, W0), vm(X0, Y0, W0), vm(X0, Y0, W0),
             vm(2, nx, ny, nz), vm(2, nx, ny, nz),
-            vm(2, X1, Y1, LANES), vm(2, 2, 3, Y1, LANES), vm(2, n1y, LANES),
+            vm(3, X1, Y1, LANES), vm(3, 2, 3, Y1, LANES), vm(3, n1y, LANES),
             vm(X1, Y1, LANES), vm(X1, Y1, LANES), vm(X1, Y1, LANES), vm(X1, Y1, LANES), vm(X1, Y1, LANES),
-            vm(2, n1x, n1y, LANES),
-            vm(3, N, 8, LANES), vm(3, 8, LANES), vm(2, N, 1, LANES), vm(2, 1, LANES),
+            vm(3, n1x, n1y, LANES),
+            vm(2, N, n2y * 3 // 2, LANES), vm(2, n2y * 3 // 2, LANES), vm(N, n2y, LANES), vm(n2y, LANES), vm(2, N, 1, LANES), vm(2, 1, LANES),
             vm(NX2 + 4, NY2, NZ2), vm(NX2 + 4, NY2, NZ2), vm(NX2 + 4, NY2, NZ2), vm(NX2 + 4, NY2, NZ2),
             vm(Y0, W0), vm(Y1, LANES),
             vb(Y1, 2 * Y0), vb(W0, LANES), vb(Y0, 2 * Y1), vb(LANES, W0),
             vb(n2y, 2 * Y1), vb(LANES, LANES), vb(Y1, 2 * NY2), vb(NZ2, LANES),
-            dma((5, 26)), dma((5, 26)), dma((5, N)), dma((5, N)),
+            dma((6, 52)), dma((6, 52)), dma((5, N)), dma((5, N)), dma((2,)),
         ]
         shape = jax.ShapeDtypeStruct(right_side.shape, F32)
         return pl.pallas_call(
             functools.partial(kernel, dims),
             out_shape=(shape, shape),
-            in_specs=[pl.BlockSpec(memory_space=pltpu.VMEM)] * 2,
+            in_specs=[pl.BlockSpec(memory_space=pl.ANY)] * 2,
             out_specs=[pl.BlockSpec(memory_space=pltpu.VMEM)] * 2,
             scratch_shapes=scratch,
-            compiler_params=pltpu.CompilerParams(has_side_effects=True),
+            compiler_params=pltpu.CompilerParams(collective_id=0, has_side_effects=True),
         )(right_side, diagonal)
 
     placed = (P("gx", "gy", "gz"), P("gx", "gy", "gz"))

time: 96.9 us -> 82.1 us (0.85)
  Pallas kernels: 93.7 us -> 78.8 us
    pallas_call x1, Pallas kernels: 93.7 us -> 78.8 us  [local(): pl.pallas_call(functools.partial(kernel, dims), out_shape=(shape, shape),...]
where the time goes in v1:
time: 82.1 us; the launch traced here: 81.9 us
  Pallas kernels  78.8 us (96%)
  local copies, waits for them, and re-layouts  2.42 us (3%)
    pallas_call x1, Pallas kernels, local(): pl.pallas_call(functools.partial(kernel, dims), out_shape=(shape, shape),...  78.8 us
    unnamed x4, local copies, waits for them, and re-layouts  2.42 us

profile of v1, /device:TPU:0, one launch (start us, length us, event | category | flops | bytes accessed | tf_op | source)
XLA Modules:
  0.0 81.9 jit_solution(698973768464078445)
XLA Ops:
  0.6 78.8 %shard_map.41 = (f32[16,32,128]{2,1,0:T(8,128)}, f32[16,32,128]{2,1,0:T(8,128)}) custom-call(f32[16,32,128]{2,1,0:T(8,128)} %x_hbm.1, f32[16,32,128]{2,1,0:T(8,128)} %d_hbm.1), custom_call_target="tpu_custom_call" | custom-call | tf_op jit(solution)/shard_map/pallas_call | solution.py:730
  79.5 0.0 copy-start
  79.5 1.7 %copy.6 = f32[16,32,128]{2,1,0:T(8,128)} copy(f32[16,32,128]{2,1,0:T(8,128)} %get-tuple-element.4) | data formatting | bytes 524288
  81.2 0.0 copy-done
  81.2 0.7 copy.7
Async XLA Ops:
  79.5 1.7 %copy-start = (f32[16,32,128]{2,1,0:T(8,128)S(1)}, f32[16,32,128]{2,1,0:T(8,128)}, u32[]{:S(2)}) copy-start(f32[16,32,128]{2,1,0:T(8,128)} %get-tuple-element.5) | copy-start | bytes 786436

commit v2 on v1

--- a/solution.py
+++ b/solution.py
@@ -1,4 +1,5 @@
 import functools
+import math
 
 import jax
 import jax.numpy as jnp
@@ -72,7 +73,7 @@
     land1, edge1, face1, D1, R1a, R1, Z1, T1, send1,
     slots, tile, eslots, etile, rows, row, G, E, Y, Q, M0, M1,
     LyR, RzR, LyP, RzP, LyR2, RzR2, LyP2, RzP2,
-    ssem, rsem, gssem, grsem, csem,
+    spare, ssem, rsem, gssem, grsem, csem,
 ):
     GX, GY, GZ = dims
     N = GX * GY * GZ
@@ -123,24 +124,22 @@
                 ok = t if ok is None else ok & t
         return ok
 
-    def remote(ex, slot, o, src, dst):
+    def remote(ex, o, src, dst):
         return pltpu.make_async_remote_copy(
-            src_ref=src, dst_ref=dst, send_sem=ssem.at[ex, slot], recv_sem=rsem.at[ex, slot],
+            src_ref=src, dst_ref=dst, send_sem=ssem.at[ex], recv_sem=rsem.at[ex],
             device_id={"gx": ix + o[0], "gy": iy + o[1], "gz": iz + o[2]}, device_id_type=MESH,
         )
 
-    def fine(e, core):
+    def fine(ex, e, core):
         def make(k, far):
             o = a, b, c = OFFSETS[k]
             ys, yd, yn = cut(b, ny, H)
-            slot = k
             if c == 0:
                 if a == 0:
                     xs, xd, xn = 0, H, nx
                 else:
                     lo, hi = (NEAR, FAR[e]) if far else (0, NEAR)
                     xs, xd, xn = (nx - hi, H - hi, hi - lo) if a > 0 else (lo, H + nx + lo, hi - lo)
-                    slot = k + far * len(OFFSETS)
                 src = core.at[pl.ds(xs, xn), pl.ds(ys, yn)]
                 dst = land.at[e, pl.ds(xd, xn), pl.ds(yd, yn)]
             else:
@@ -149,7 +148,7 @@
                     src, dst = face.at[e, f, pl.ds(ys, yn)], edge.at[e, side, 1, pl.ds(yd, yn)]
                 else:
                     src, dst = corner.at[e, (1 - a) // 2, f], cland.at[e, side, (1 - a) // 2, 1 - b]
-            return remote(e, slot, o, src, dst)
+            return ex + far, o, src, dst
         return make
 
     def level1(ex, e, h):
@@ -162,7 +161,7 @@
                 dst = land1.at[e, pl.ds(xd, xn), pl.ds(yd, yn)]
             else:
                 src, dst = face1.at[e, pl.ds(ys, yn)], edge1.at[e, 0 if c > 0 else 1, 1 - a, pl.ds(yd, yn)]
-            return remote(ex, k, o, src, dst)
+            return ex, o, src, dst
         return make
 
     FLAT = [k for k, o in enumerate(OFFSETS) if o[2] == 0]
@@ -175,23 +174,43 @@
             @pl.when(there(OFFSETS[k], 1))
             def _():
                 for make in makers:
-                    make(k, far).start()
+                    remote(*make(k, far)).start()
+
+    def counts(i, g):
+        if g < 3:
+            return [(g - 1, None)]
+        outer = (i == 0) | (i == g - 1)
+        return [(1, outer), (2, jnp.logical_not(outer))]
+
+    def settle(makers, ks, far, received):
+        for cx, px in counts(ix, GX):
+            for cy, py in counts(iy, GY):
+                for cz, pz in counts(iz, GZ):
+                    n = 0
+                    for k in ks:
+                        a, b, c = OFFSETS[k]
+                        if min(a, b, c) >= 0:
+                            times = (cx if a else 1) * (cy if b else 1) * (cz if c else 1)
+                            for make in makers:
+                                n += times * math.prod(make(k, far)[2].shape) // (H * LANES)
+                    if n == 0:
+                        continue
+                    some = spare.at[pl.ds(0, n)]
+                    copy = remote(makers[0](0, far)[0], (0, 0, 1), some, some)
+                    wait = copy.wait_recv if received else copy.wait_send
+                    ok = [p for p in (px, py, pz) if p is not None]
+                    if ok:
+                        pl.when(functools.reduce(jnp.logical_and, ok))(wait)
+                    else:
+                        wait()
+
+    def finish(makers, ks, far=0):
+        settle(makers, ks, far, True)
         sent.append((makers, ks, far))
-
-    def finish(makers, ks, far=0):
-        for k in ks:
-            @pl.when(there(OFFSETS[k], -1))
-            def _():
-                for make in makers:
-                    make(k, far).wait_recv()
 
     def drain():
         for makers, ks, far in sent:
-            for k in ks:
-                @pl.when(there(OFFSETS[k], 1))
-                def _():
-                    for make in makers:
-                        make(k, far).wait_send()
+            settle(makers, ks, far, False)
 
     def ends(k, sender):
         if k == 0:
@@ -200,34 +219,31 @@
             return tile.at[k - 1], slots.at[k - 1, sender]
         return row.at[k - 3], rows.at[k - 3, sender]
 
-    def gather_copy(k, send_slot, sender, target):
-        src, dst = ends(k, sender)
-        return pltpu.make_async_remote_copy(
-            src_ref=src, dst_ref=dst,
-            send_sem=gssem.at[k, send_slot], recv_sem=grsem.at[k, sender],
-            device_id=device(target), device_id_type=MESH,
-        )
-
     def gather_start(k):
+        src, dst = ends(k, me)
+
         def body(d, _):
-            gather_copy(k, d, me, (me + d) % N).start()
+            pltpu.make_async_remote_copy(
+                src_ref=src, dst_ref=dst, send_sem=gssem.at[k], recv_sem=grsem.at[k],
+                device_id=device((me + d) % N), device_id_type=MESH,
+            ).start()
             return 0
         lax.fori_loop(1, N, body, 0)
-        src, dst = ends(k, me)
         dst[...] = src[...]
 
+    def everyone(k):
+        some = pl.ds(0, N - 1)
+        ref = eslots.at[some] if k == 0 else slots.at[k - 1, some] if k < 3 else rows.at[k - 3, some]
+        return pltpu.make_async_remote_copy(
+            src_ref=ref, dst_ref=ref, send_sem=gssem.at[k], recv_sem=grsem.at[k],
+            device_id=device((me + 1) % N), device_id_type=MESH,
+        )
+
     def gather_finish(k):
-        def body(d, _):
-            s = (me + N - d) % N
-            gather_copy(k, d, s, s).wait_recv()
-            return 0
-        lax.fori_loop(1, N, body, 0)
+        everyone(k).wait_recv()
 
     def gather_drain(k):
-        def body(d, _):
-            gather_copy(k, d, me, me).wait_send()
-            return 0
-        lax.fori_loop(1, N, body, 0)
+        everyone(k).wait_send()
 
     lane = iota((1, LANES), 1)
 
@@ -262,7 +278,7 @@
     pl.semaphore_wait(barrier, N - 1)
     for load in loads:
         load.wait()
-    both = [fine(0, d_ref), fine(1, x_ref)]
+    both = [fine(0, 0, d_ref), fine(0, 1, x_ref)]
     start(both, FLAT)
     pack0(0, d_ref)
     pack0(1, x_ref)
@@ -369,8 +385,7 @@
     def put_r(p, v):
         return put(R, p, v)
 
-    finish(both, FLAT)
-    finish(both, PACKED)
+    finish(both, FLAT + PACKED)
     merge0(0, d_ref, put_d)
     merge0(1, x_ref, put_r)
 
@@ -409,7 +424,7 @@
             loop(lo, hi, body, 5)
 
     pack1(2, D1)
-    start([level1(3, 2, 4)], FLAT + PACKED)
+    start([level1(6, 2, 4)], FLAT + PACKED)
 
     def coarse_tile(s):
         return mr(ml(LyR2, s), RzR2)
@@ -562,7 +577,7 @@
         finish(fine1, FLAT + PACKED)
         merge1(it, 5, R1)
         if it == 0:
-            finish([level1(3, 2, 4)], FLAT + PACKED)
+            finish([level1(6, 2, 4)], FLAT + PACKED)
             merge1(2, 4, D1, False)
 
         def z1b(p):
@@ -663,15 +678,14 @@
 
     precondition(0)
     products(0)
-    image = [fine(2, W.at[0])]
+    image = [fine(2, 2, W.at[0])]
     start(image, FLAT)
     pack0(2, W.at[0])
     start(image, PACKED)
     start(image, WIDER, 1)
     rz0, curve0, _ = total(3)
     alpha0 = rz0 / curve0
-    finish(image, FLAT)
-    finish(image, PACKED)
+    finish(image, FLAT + PACKED)
 
     def put_image(p, v):
         return put(R, p, R[p] - alpha0 * v)
@@ -724,7 +738,7 @@
             vm(Y0, W0), vm(Y1, LANES),
             vb(Y1, 2 * Y0), vb(W0, LANES), vb(Y0, 2 * Y1), vb(LANES, W0),
             vb(n2y, 2 * Y1), vb(LANES, LANES), vb(Y1, 2 * NY2), vb(NZ2, LANES),
-            dma((6, 52)), dma((6, 52)), dma((5, N)), dma((5, N)), dma((2,)),
+            vm(256, H, LANES), dma((7,)), dma((7,)), dma((5,)), dma((5,)), dma((2,)),
         ]
         shape = jax.ShapeDtypeStruct(right_side.shape, F32)
         return pl.pallas_call(

time: 82.1 us -> 71.7 us (0.87)
  Pallas kernels: 78.8 us -> 68.5 us
    pallas_call x1, Pallas kernels: 78.8 us -> 68.5 us  [local(): pl.pallas_call(functools.partial(kernel, dims), out_shape=(shape, shape),...]
where the time goes in v2:
time: 71.7 us; the launch traced here: 71.5 us
  Pallas kernels  68.5 us (96%)
  local copies, waits for them, and re-layouts  2.42 us (3%)
    pallas_call x1, Pallas kernels, local(): pl.pallas_call(functools.partial(kernel, dims), out_shape=(shape, shape),...  68.5 us
    unnamed x4, local copies, waits for them, and re-layouts  2.42 us

profile of v2, /device:TPU:0, one launch (start us, length us, event | category | flops | bytes accessed | tf_op | source)
XLA Modules:
  0.0 71.5 jit_solution(9798194556114420876)
XLA Ops:
  0.6 68.5 %shard_map.41 = (f32[16,32,128]{2,1,0:T(8,128)}, f32[16,32,128]{2,1,0:T(8,128)}) custom-call(f32[16,32,128]{2,1,0:T(8,128)} %x_hbm.1, f32[16,32,128]{2,1,0:T(8,128)} %d_hbm.1), custom_call_target="tpu_custom_call" | custom-call | tf_op jit(solution)/shard_map/pallas_call | solution.py:744
  69.1 0.0 copy-start
  69.1 1.7 %copy.6 = f32[16,32,128]{2,1,0:T(8,128)} copy(f32[16,32,128]{2,1,0:T(8,128)} %get-tuple-element.4) | data formatting | bytes 524288
  70.8 0.0 copy-done
  70.8 0.7 copy.7
Async XLA Ops:
  69.1 1.7 %copy-start = (f32[16,32,128]{2,1,0:T(8,128)S(1)}, f32[16,32,128]{2,1,0:T(8,128)}, u32[]{:S(2)}) copy-start(f32[16,32,128]{2,1,0:T(8,128)} %get-tuple-element.5) | copy-start | bytes 786436

commit v3 on v2

--- a/solution.py
+++ b/solution.py
@@ -12,7 +12,7 @@
 LANES = 128
 H = 8
 MESH = pl.DeviceIdType.MESH
-F32, BF16 = jnp.float32, jnp.bfloat16
+F32 = jnp.float32
 UF, UR, U1, UC, UM, UP = 4, 4, 4, 8, 4, 4
 OFFSETS = [
     (a, b, c) for a in (-1, 0, 1) for b in (-1, 0, 1) for c in (-1, 0, 1) if (a, b, c) != (0, 0, 0)
@@ -37,20 +37,8 @@
     return k2, k3
 
 
-def halves(v):
-    high = v.astype(BF16)
-    return high, (v - high.astype(F32)).astype(BF16)
-
-
-def ml(m, v):
-    return lax.dot(m[...], jnp.concatenate(halves(v), axis=0), preferred_element_type=F32)
-
-
-def mr(v, m):
-    high, low = halves(v)
-    return lax.dot(high, m[...], preferred_element_type=F32) + lax.dot(
-        low, m[...], preferred_element_type=F32
-    )
+def take(v, index):
+    return jnp.take_along_axis(v, jnp.broadcast_to(index, v.shape), axis=1, mode="promise_in_bounds")
 
 
 def iota(shape, dim):
@@ -71,8 +59,7 @@
     dims, x_hbm, d_hbm, sol_ref, res_ref,
     x_ref, d_ref, land, edge, face, corner, cland, D, R, Z, T, W, S0,
     land1, edge1, face1, D1, R1a, R1, Z1, T1, send1,
-    slots, tile, eslots, etile, rows, row, G, E, Y, Q, M0, M1,
-    LyR, RzR, LyP, RzP, LyR2, RzR2, LyP2, RzP2,
+    slots, tile, eslots, etile, rows, row, G, E, Y, Q, QP, S, M0, M1,
     spare, ssem, rsem, gssem, grsem, csem,
 ):
     GX, GY, GZ = dims
@@ -291,18 +278,12 @@
     def off1(l):
         return jnp.where(l < 96, l, l - 128)
 
-    def pair(fine, coarse):
-        return (fine == 2 * coarse) | (fine == 2 * coarse + 1)
-
     def inside(v, i, n, g):
         v = v + i * n
         return (v >= 0) & (v < g * n)
 
     def f(cond, value=1.0):
         return jnp.where(cond, F32(value), F32(0.0))
-
-    def twice(m):
-        return jnp.concatenate([m, m], axis=1).astype(BF16)
 
     def near0(z):
         return (z >= -H) & (z < nz + H)
@@ -314,22 +295,31 @@
     M0[...] = f(inside(yy, iy, ny, GY) & inside(zz, iz, nz, GZ) & near0(zz))
     yy, zz = iota((Y1, LANES), 0) - H, off1(iota((Y1, LANES), 1))
     M1[...] = f(inside(yy, iy, n1y, GY) & inside(zz, iz, n1z, GZ) & near1(zz))
-    c, v = iota((Y1, Y0), 0) - H, iota((Y1, Y0), 1) - H
-    LyR[...] = twice(f(pair(v, c) & inside(c, iy, n1y, GY), 0.5))
-    v, c = iota((Y0, Y1), 0) - H, iota((Y0, Y1), 1) - H
-    LyP[...] = twice(f(pair(v, c) & inside(c, iy, n1y, GY)))
-    v, c = off0(iota((W0, LANES), 0)), off1(iota((W0, LANES), 1))
-    RzR[...] = f(pair(v, c) & inside(c, iz, n1z, GZ) & near0(v)).astype(BF16)
-    c, v = off1(iota((LANES, W0), 0)), off0(iota((LANES, W0), 1))
-    RzP[...] = f(pair(v, c) & inside(c, iz, n1z, GZ) & near0(v)).astype(BF16)
-    c, v = iota((n2y, Y1), 0), iota((n2y, Y1), 1) - H
-    LyR2[...] = twice(f(pair(v, c), 0.5))
-    v, c = off1(iota((LANES, LANES), 0)), iota((LANES, LANES), 1) % n2z
-    RzR2[...] = f(pair(v, c)).astype(BF16)
-    v, c = iota((Y1, NY2), 0) - H + iy * n1y, iota((Y1, NY2), 1)
-    LyP2[...] = twice(f(pair(v, c)))
-    c, v = iota((NZ2, LANES), 0), off1(iota((NZ2, LANES), 1))
-    RzP2[...] = f(pair(v + iz * n1z, c) & near1(v)).astype(BF16)
+    everywhere = iota((1, LANES), 1)
+    evens, halved = everywhere * 2 % LANES, everywhere // 2
+    blocks = everywhere % n2z * 2
+    MID = slice(H // 2, H // 2 + Y0 // 2)
+
+    def put_halves(p, v):
+        def store():
+            S[0, p] = v[:, :LANES]
+            S[1, p] = v[:, LANES:]
+        return store
+
+    def shrink0(p):
+        def half(h):
+            v = S[h, p, pl.ds(0, Y0 // 2, stride=2)] + S[h, p, pl.ds(1, Y0 // 2, stride=2)]
+            return take(v + pltpu.roll(v, LANES - 1, 1), evens)
+        return jnp.where(everywhere < n1z, half(0), half(1))
+
+    def put_mid(ref, p, v):
+        def store():
+            ref[p, MID] = v
+        return store
+
+    def shrink1(src, p):
+        v = src[p, pl.ds(H, n2y, stride=2)] + src[p, pl.ds(H + 1, n2y, stride=2)]
+        return 0.5 * take(v + pltpu.roll(v, LANES - 1, 1), blocks)
 
     def xin0(p):
         return f(inside(p - H, ix, nx, GX))
@@ -376,8 +366,9 @@
             loop(lo, hi, body, UM)
 
     none = jnp.zeros((2, Y1, LANES), F32)
-    R1a[H - 2 : H] = none
-    R1a[H + n1x : H + n1x + 2] = none
+    R1a[...] = jnp.zeros(R1a.shape, F32)
+    D1[...] = jnp.zeros(D1.shape, F32)
+    QP[...] = jnp.zeros(QP.shape, F32)
 
     def put_d(p, v):
         return put(D, p, v)
@@ -389,10 +380,13 @@
     merge0(0, d_ref, put_d)
     merge0(1, x_ref, put_r)
 
+    def pair_d(p):
+        return put_halves(p, D[2 * p - H] + D[2 * p - H + 1])
+
     def make_d1(p):
-        s = D[2 * p - H] + D[2 * p - H + 1]
-        return put(D1, p, 0.25 * mr(ml(LyR, s), RzR))
-
+        return put_mid(D1, p, 0.125 * shrink0(p))
+
+    loop(H - 1, H + n1x + 1, pair_d, 5)
     loop(H - 1, H + n1x + 1, make_d1, 5)
 
     def pack1(e, src):
@@ -426,14 +420,12 @@
     pack1(2, D1)
     start([level1(6, 2, 4)], FLAT + PACKED)
 
-    def coarse_tile(s):
-        return mr(ml(LyR2, s), RzR2)
-
     def coarsen(plane):
         total = jnp.zeros((n2y, LANES), F32)
         for x in range(n2x):
-            v = coarse_tile(plane(H + 2 * x) + plane(H + 2 * x + 1))
-            total = total + jnp.where((lane >= n2z * x) & (lane < n2z * x + n2z), v, 0.0)
+            T1[x] = plane(H + 2 * x) + plane(H + 2 * x + 1)
+        for x in range(n2x):
+            total = total + jnp.where((lane >= n2z * x) & (lane < n2z * x + n2z), shrink1(T1, x), 0.0)
         return total
 
     etile[...] = coarsen(lambda p: D1[p]) * 0.25
@@ -522,7 +514,9 @@
             y = Y[p]
             left = G[p] - ((27.0 + E[p]) * y - box2(Y, p))
             shift = jnp.sum(left, axis=1, keepdims=True) / jnp.sum(1.0 + E[p], axis=1, keepdims=True)
-            return put(Q, p, y + shift)
+            def store():
+                QP[p, H : H + NY2] = y + shift
+            return store
 
         for body in (first, second, third):
             loop(2, NX2 + 2, body, UC)
@@ -541,11 +535,14 @@
         def rest0(p):
             return R[p] - ((27.0 + D[p]) * Z[p] - box(Z, p))
 
+        def pair0(p):
+            return put_halves(p, rest0(2 * p - H) + rest0(2 * p - H + 1))
+
         def down1(p):
-            s = rest0(2 * p - H) + rest0(2 * p - H + 1)
-            return put(R1a, p, mr(ml(LyR, s), RzR))
-
-        loop(H, H + n1x, down1, UR)
+            return put_mid(R1a, p, 0.5 * M1[MID] * shrink0(p))
+
+        loop(H, H + n1x, pair0, 2)
+        loop(H, H + n1x, down1, 8)
 
         pack1(it, R1a)
         fine1 = [level1(ex, it, 5)]
@@ -563,8 +560,9 @@
             return R1a[p] - ((27.0 + D1[p]) * Z1[p] - box(Z1, p))
 
         tile[it, 0:n2y] = coarsen(rest1)
-        low = coarse_tile(box(Z1, H - 2) + rest1(H - 1))
-        high = coarse_tile(rest1(H + n1x) + box(Z1, H + n1x + 1))
+        T1[n2x] = box(Z1, H - 2) + rest1(H - 1)
+        T1[n2x + 1] = rest1(H + n1x) + box(Z1, H + n1x + 1)
+        low, high = shrink1(T1, n2x), shrink1(T1, n2x + 1)
         low, high = (jnp.where(lane < 2 * n2z, v, pltpu.roll(v, n2y // 2, 0)) for v in (low, high))
         ring2 = jnp.where(lane // n2z % 2 == 0, low, high)
         tile[it, n2y : n2y + n2y // 2] = ring2[0 : n2y // 2]
@@ -592,12 +590,30 @@
         spread(lambda n, r: slots[it, n, n2y:] if r else slots[it, n, 0:n2y], G, True)
         coarse()
 
+        zz = off1(everywhere)
+        source = (zz + iz * n1z) // 2
+        fits = inside(zz, iz, n1z, GZ) & near1(zz)
+
+        def wide1(q):
+            rows2 = pl.ds(pl.multiple_of(iy * n2y, H), n2y + 2 * H)
+            v = jnp.zeros((n1y, LANES), F32)
+            for t in range(NZ2 // LANES):
+                part = QP[ix * n2x + q, rows2, LANES * t : LANES * t + LANES][H // 2 : H // 2 + n1y]
+                at = source - LANES * t
+                v = jnp.where(fits & (at >= 0) & (at < LANES), take(part, jnp.clip(at, 0, LANES - 1)), v)
+
+            def store():
+                T1[q, pl.ds(0, n1y, stride=2)] = v
+                T1[q, pl.ds(1, n1y, stride=2)] = v
+            return store
+
         def up1(q):
-            v = mr(ml(LyP2, Q[ix * n2x + q]), RzP2)
+            v = T1[q]
             p = H - 4 + 2 * q
             a, b = put(Z1, p, Z1[p] + v), put(Z1, p + 1, Z1[p + 1] + v)
             return lambda: (a(), b())
 
+        loop(0, n2x + 4, wide1, 8)
         loop(0, n2x + 4, up1, 4)
 
         def t1(p):
@@ -610,13 +626,24 @@
 
         loop(H - 2, H + n1x + 2, z1c, U1)
 
+        def wide0(p):
+            v = Z1[p, MID]
+            parts = take(v, halved), take(v, halved + n1z)
+
+            def store():
+                for h, part in enumerate(parts):
+                    S[h, p, pl.ds(0, Y0 // 2, stride=2)] = part
+                    S[h, p, pl.ds(1, Y0 // 2, stride=2)] = part
+            return store
+
         def up0(p):
-            v = mr(ml(LyP, Z1[p]), RzP)
+            v = jnp.concatenate([S[0, p], S[1, p]], axis=1)
             q = 2 * p - H
             a, b = put(Z, q, Z[q] + v), put(Z, q + 1, Z[q + 1] + v)
             return lambda: (a(), b())
 
-        loop(H - 2, H + n1x + 2, up0, UR)
+        loop(H - 2, H + n1x + 2, wide0, 4)
+        loop(H - 2, H + n1x + 2, up0, 4)
 
         def t0(p):
             return put(T, p, (M0[...] * xin0(p)) * rest0(p))
@@ -722,7 +749,6 @@
         NX2, NY2, NZ2 = dims[0] * nx // 4, dims[1] * n2y, dims[2] * nz // 4
         W0 = 2 * LANES
         vm = lambda *s: pltpu.VMEM(s, F32)
-        vb = lambda *s: pltpu.VMEM(s, BF16)
         dma = pltpu.SemaphoreType.DMA
         scratch = [
             vm(nx, ny, nz), vm(nx, ny, nz),
@@ -735,9 +761,7 @@
             vm(3, n1x, n1y, LANES),
             vm(2, N, n2y * 3 // 2, LANES), vm(2, n2y * 3 // 2, LANES), vm(N, n2y, LANES), vm(n2y, LANES), vm(2, N, 1, LANES), vm(2, 1, LANES),
             vm(NX2 + 4, NY2, NZ2), vm(NX2 + 4, NY2, NZ2), vm(NX2 + 4, NY2, NZ2), vm(NX2 + 4, NY2, NZ2),
-            vm(Y0, W0), vm(Y1, LANES),
-            vb(Y1, 2 * Y0), vb(W0, LANES), vb(Y0, 2 * Y1), vb(LANES, W0),
-            vb(n2y, 2 * Y1), vb(LANES, LANES), vb(Y1, 2 * NY2), vb(NZ2, LANES),
+            vm(NX2 + 4, NY2 + 2 * H, NZ2), vm(2, X0, Y0, LANES), vm(Y0, W0), vm(Y1, LANES),
             vm(256, H, LANES), dma((7,)), dma((7,)), dma((5,)), dma((5,)), dma((2,)),
         ]
         shape = jax.ShapeDtypeStruct(right_side.shape, F32)

time: 71.7 us -> 66.3 us (0.925)
  Pallas kernels: 68.5 us -> 63 us
    pallas_call x1, Pallas kernels: 68.5 us -> 63 us  [local(): pl.pallas_call(functools.partial(kernel, dims), out_shape=(shape, shape),...]
where the time goes in v3:
time: 66.3 us; the launch traced here: 66.1 us
  Pallas kernels  63 us (95%)
  local copies, waits for them, and re-layouts  2.42 us (4%)
    pallas_call x1, Pallas kernels, local(): pl.pallas_call(functools.partial(kernel, dims), out_shape=(shape, shape),...  63 us
    unnamed x4, local copies, waits for them, and re-layouts  2.42 us

profile of v3, /device:TPU:0, one launch (start us, length us, event | category | flops | bytes accessed | tf_op | source)
XLA Modules:
  0.0 66.1 jit_solution(15114505385199365865)
XLA Ops:
  0.6 63.0 %shard_map.41 = (f32[16,32,128]{2,1,0:T(8,128)}, f32[16,32,128]{2,1,0:T(8,128)}) custom-call(f32[16,32,128]{2,1,0:T(8,128)} %x_hbm.1, f32[16,32,128]{2,1,0:T(8,128)} %d_hbm.1), custom_call_target="tpu_custom_call" | custom-call | tf_op jit(solution)/shard_map/pallas_call | solution.py:768
  63.7 0.0 copy-start
  63.7 1.7 %copy.6 = f32[16,32,128]{2,1,0:T(8,128)} copy(f32[16,32,128]{2,1,0:T(8,128)} %get-tuple-element.4) | data formatting | bytes 524288
  65.4 0.0 copy-done
  65.4 0.7 %copy.7 = f32[16,32,128]{2,1,0:T(8,128)} copy(f32[16,32,128]{2,1,0:T(8,128)S(1)} %copy-done) | data formatting | bytes 524288
Async XLA Ops:
  63.7 1.7 %copy-start = (f32[16,32,128]{2,1,0:T(8,128)S(1)}, f32[16,32,128]{2,1,0:T(8,128)}, u32[]{:S(2)}) copy-start(f32[16,32,128]{2,1,0:T(8,128)} %get-tuple-element.5) | copy-start | bytes 786436

commit v4 on v3

--- a/solution.py
+++ b/solution.py
@@ -13,7 +13,7 @@
 H = 8
 MESH = pl.DeviceIdType.MESH
 F32 = jnp.float32
-UF, UR, U1, UC, UM, UP = 4, 4, 4, 8, 4, 4
+UF, UR, U1, UC, UM, UP = 4, 4, 4, 6, 4, 4
 OFFSETS = [
     (a, b, c) for a in (-1, 0, 1) for b in (-1, 0, 1) for c in (-1, 0, 1) if (a, b, c) != (0, 0, 0)
 ]
@@ -59,7 +59,7 @@
     dims, x_hbm, d_hbm, sol_ref, res_ref,
     x_ref, d_ref, land, edge, face, corner, cland, D, R, Z, T, W, S0,
     land1, edge1, face1, D1, R1a, R1, Z1, T1, send1,
-    slots, tile, eslots, etile, rows, row, G, E, Y, Q, QP, S, M0, M1,
+    slots, tile, eslots, etile, rows, row, G, E, Y, Q, QP, lines, S, M0, M1,
     spare, ssem, rsem, gssem, grsem, csem,
 ):
     GX, GY, GZ = dims
@@ -79,7 +79,8 @@
     DEEP = LANES // ny
 
     def device(n):
-        return {"gx": n // (GY * GZ), "gy": (n // GZ) % GY, "gz": n % GZ}
+        n = lax.rem(n, N)
+        return {"gx": lax.div(n, GY * GZ), "gy": lax.rem(lax.div(n, GZ), GY), "gz": lax.rem(n, GZ)}
 
     loads = [
         pltpu.make_async_copy(src, dst, csem.at[i])
@@ -88,7 +89,7 @@
     barrier = pltpu.get_barrier_semaphore()
 
     def greet(d, _):
-        pl.semaphore_signal(barrier, inc=1, device_id=device((me + d) % N), device_id_type=MESH)
+        pl.semaphore_signal(barrier, inc=1, device_id=device(me + d), device_id_type=MESH)
         return 0
 
     lax.fori_loop(1, N, greet, 0)
@@ -212,7 +213,7 @@
         def body(d, _):
             pltpu.make_async_remote_copy(
                 src_ref=src, dst_ref=dst, send_sem=gssem.at[k], recv_sem=grsem.at[k],
-                device_id=device((me + d) % N), device_id_type=MESH,
+                device_id=device(me + d), device_id_type=MESH,
             ).start()
             return 0
         lax.fori_loop(1, N, body, 0)
@@ -223,7 +224,7 @@
         ref = eslots.at[some] if k == 0 else slots.at[k - 1, some] if k < 3 else rows.at[k - 3, some]
         return pltpu.make_async_remote_copy(
             src_ref=ref, dst_ref=ref, send_sem=gssem.at[k], recv_sem=grsem.at[k],
-            device_id=device((me + 1) % N), device_id_type=MESH,
+            device_id=device(me + 1), device_id_type=MESH,
         )
 
     def gather_finish(k):
@@ -513,13 +514,22 @@
         def third(p):
             y = Y[p]
             left = G[p] - ((27.0 + E[p]) * y - box2(Y, p))
-            shift = jnp.sum(left, axis=1, keepdims=True) / jnp.sum(1.0 + E[p], axis=1, keepdims=True)
+            shift = jnp.sum(left, axis=1, keepdims=True) * lines[p][:, 0:1]
+
             def store():
                 QP[p, H : H + NY2] = y + shift
             return store
 
-        for body in (first, second, third):
-            loop(2, NX2 + 2, body, UC)
+        for body, reach in ((first, 4), (second, 3), (third, 2)):
+            count = min(n2x + 2 * reach, NX2)
+            base = jnp.clip(ix * n2x - reach, 0, NX2 - count) + 2
+            loop(0, count, lambda p: body(base + p), UC)
+
+    def line_sums():
+        def body(p):
+            v = 1.0 / jnp.sum(1.0 + E[p], axis=1, keepdims=True)
+            return put(lines, p, jnp.broadcast_to(v, (NY2, LANES)))
+        loop(2, NX2 + 2, body, UC)
 
     def smooth1(ref, p):
         return ref[p] * (k3 - k2 * D1[p]) + k2 * box(ref, p)
@@ -586,6 +596,7 @@
         if it == 0:
             gather_finish(0)
             spread(lambda n, r: eslots[n], E, False)
+            line_sums()
         gather_finish(1 + it)
         spread(lambda n, r: slots[it, n, n2y:] if r else slots[it, n, 0:n2y], G, True)
         coarse()
@@ -761,10 +772,10 @@
             vm(3, n1x, n1y, LANES),
             vm(2, N, n2y * 3 // 2, LANES), vm(2, n2y * 3 // 2, LANES), vm(N, n2y, LANES), vm(n2y, LANES), vm(2, N, 1, LANES), vm(2, 1, LANES),
             vm(NX2 + 4, NY2, NZ2), vm(NX2 + 4, NY2, NZ2), vm(NX2 + 4, NY2, NZ2), vm(NX2 + 4, NY2, NZ2),
-            vm(NX2 + 4, NY2 + 2 * H, NZ2), vm(2, X0, Y0, LANES), vm(Y0, W0), vm(Y1, LANES),
+            vm(NX2 + 4, NY2 + 2 * H, NZ2), vm(NX2 + 4, NY2, LANES), vm(2, X0, Y0, LANES), vm(Y0, W0), vm(Y1, LANES),
             vm(256, H, LANES), dma((7,)), dma((7,)), dma((5,)), dma((5,)), dma((2,)),
         ]
-        shape = jax.ShapeDtypeStruct(right_side.shape, F32)
+        shape = pltpu.VMEM(right_side.shape, F32)
         return pl.pallas_call(
             functools.partial(kernel, dims),
             out_shape=(shape, shape),

time: 66.3 us -> 63.4 us (0.956)
  Pallas kernels: 63 us -> 61.2 us
  local copies, waits for them, and re-layouts: 2.42 us -> 1.41 us
    pallas_call x1, Pallas kernels: 63 us -> 61.2 us  [local(): pl.pallas_call(functools.partial(kernel, dims), out_shape=(shape, shape),...]
    unnamed x4 -> x2, local copies, waits for them, and re-layouts: 2.42 us -> 1.41 us
where the time goes in v4:
time: 63.4 us; the launch traced here: 63.3 us
  Pallas kernels  61.2 us (97%)
  local copies, waits for them, and re-layouts  1.41 us (2%)
  between operations  0.64 us (1%)
    pallas_call x1, Pallas kernels, local(): pl.pallas_call(functools.partial(kernel, dims), out_shape=(shape, shape),...  61.2 us
    unnamed x2, local copies, waits for them, and re-layouts  1.41 us

profile of v4, /device:TPU:0, one launch (start us, length us, event | category | flops | bytes accessed | tf_op | source)
XLA Modules:
  0.0 63.3 jit_solution(18065113475209930988)
XLA Ops:
  0.6 61.2 %shard_map.41 = (f32[16,32,128]{2,1,0:T(8,128)S(1)}, f32[16,32,128]{2,1,0:T(8,128)S(1)}) custom-call(f32[16,32,128]{2,1,0:T(8,128)} %x_hbm.1, f32[16,32,128]{2,1,0:T(8,128)} %d_hbm.1), custom_call_target="tpu_custom_call" | custom-call | tf_op jit(solution)/shard_map/pallas_call | solution.py:779
  61.9 0.7 %copy.6 = f32[16,32,128]{2,1,0:T(8,128)} copy(f32[16,32,128]{2,1,0:T(8,128)S(1)} %get-tuple-element.2) | data formatting | bytes 524288
  62.6 0.7 %copy.7 = f32[16,32,128]{2,1,0:T(8,128)} copy(f32[16,32,128]{2,1,0:T(8,128)S(1)} %get-tuple-element.3) | data formatting | bytes 524288

commit v5 on v4

--- a/solution.py
+++ b/solution.py
@@ -13,7 +13,7 @@
 H = 8
 MESH = pl.DeviceIdType.MESH
 F32 = jnp.float32
-UF, UR, U1, UC, UM, UP = 4, 4, 4, 6, 4, 4
+UF, UR, U1, UC, UM, UP = 4, 8, 8, 12, 8, 4
 OFFSETS = [
     (a, b, c) for a in (-1, 0, 1) for b in (-1, 0, 1) for c in (-1, 0, 1) if (a, b, c) != (0, 0, 0)
 ]
@@ -453,7 +453,7 @@
                         v = along(lambda q: load((a * GY + b) * GZ + t * PER + q, 0), x)
                         dst[a * n2x + x + 2, n2y * b : n2y * b + n2y, LANES * t : LANES * t + LANES] = v
             return lambda: None
-        loop(0, GX, body)
+        loop(0, GX, body, GX)
         if not ring:
             return
 
@@ -467,7 +467,7 @@
                         at = (p, slice(n2y * b, n2y * b + n2y), slice(LANES * t, LANES * t + LANES))
                         dst[at] = dst[at] + v
             return lambda: None
-        loop(0, GX, edges)
+        loop(0, GX, edges, GX)
         zero = jnp.zeros((NY2, NZ2), F32)
         dst[1] = zero
         dst[NX2 + 2] = zero
@@ -551,12 +551,11 @@
         def down1(p):
             return put_mid(R1a, p, 0.5 * M1[MID] * shrink0(p))
 
-        loop(H, H + n1x, pair0, 2)
+        loop(H, H + n1x, pair0, 4)
         loop(H, H + n1x, down1, 8)
 
         pack1(it, R1a)
         fine1 = [level1(ex, it, 5)]
-        start(fine1, FLAT + PACKED)
 
         Z1[H - 3 : H - 1] = none
         Z1[H + n1x + 1 : H + n1x + 3] = none
@@ -577,21 +576,11 @@
         ring2 = jnp.where(lane // n2z % 2 == 0, low, high)
         tile[it, n2y : n2y + n2y // 2] = ring2[0 : n2y // 2]
         gather_start(1 + it)
+        start(fine1, FLAT + PACKED)
 
         far(it)
         for lo, hi in ((H - 3, H - 1), (H + nx + 1, H + nx + 3)):
             loop(lo, hi, down0, 2)
-
-        finish(fine1, FLAT + PACKED)
-        merge1(it, 5, R1)
-        if it == 0:
-            finish([level1(6, 2, 4)], FLAT + PACKED)
-            merge1(2, 4, D1, False)
-
-        def z1b(p):
-            return put(Z1, p, (M1[...] * xin1(p)) * smooth1(R1, p))
-
-        loop(H - 4, H + n1x + 4, z1b, U1)
 
         if it == 0:
             gather_finish(0)
@@ -600,6 +589,17 @@
         gather_finish(1 + it)
         spread(lambda n, r: slots[it, n, n2y:] if r else slots[it, n, 0:n2y], G, True)
         coarse()
+        finish(fine1, FLAT + PACKED)
+        merge1(it, 5, R1)
+        if it == 0:
+            finish([level1(6, 2, 4)], FLAT + PACKED)
+            merge1(2, 4, D1, False)
+
+        def z1b(p):
+            return put(Z1, p, (M1[...] * xin1(p)) * smooth1(R1, p))
+
+        loop(H - 4, H + n1x + 4, z1b, U1)
+
 
         zz = off1(everywhere)
         source = (zz + iz * n1z) // 2
@@ -625,17 +625,17 @@
             return lambda: (a(), b())
 
         loop(0, n2x + 4, wide1, 8)
-        loop(0, n2x + 4, up1, 4)
+        loop(0, n2x + 4, up1, 8)
 
         def t1(p):
             return put(T1, p, (M1[...] * xin1(p)) * (R1[p] - ((27.0 + D1[p]) * Z1[p] - box(Z1, p))))
 
-        loop(H - 3, H + n1x + 3, t1, U1)
+        loop(H - 3, H + n1x + 3, t1, 7)
 
         def z1c(p):
             return put(Z1, p, Z1[p] + (M1[...] * xin1(p)) * smooth1(T1, p))
 
-        loop(H - 2, H + n1x + 2, z1c, U1)
+        loop(H - 2, H + n1x + 2, z1c, 6)
 
         def wide0(p):
             v = Z1[p, MID]
@@ -653,18 +653,18 @@
             a, b = put(Z, q, Z[q] + v), put(Z, q + 1, Z[q + 1] + v)
             return lambda: (a(), b())
 
-        loop(H - 2, H + n1x + 2, wide0, 4)
-        loop(H - 2, H + n1x + 2, up0, 4)
+        loop(H - 2, H + n1x + 2, wide0, 12)
+        loop(H - 2, H + n1x + 2, up0, 6)
 
         def t0(p):
             return put(T, p, (M0[...] * xin0(p)) * rest0(p))
 
-        loop(H - 2, H + nx + 2, t0, UF)
+        loop(H - 2, H + nx + 2, t0, 5)
 
         def z0(p):
             return put(Z, p, Z[p] + (M0[...] * xin0(p)) * (T[p] * (k3 - k2 * D[p]) + k2 * box(T, p)))
 
-        loop(H - 1, H + nx + 1, z0, UF)
+        loop(H - 1, H + nx + 1, z0, 6)
 
     core = (slice(H, H + ny), slice(0, nz))
 

time: 63.4 us -> 58.9 us (0.929)
  Pallas kernels: 61.2 us -> 56.7 us
    pallas_call x1, Pallas kernels: 61.2 us -> 56.7 us  [local(): pl.pallas_call(functools.partial(kernel, dims), out_shape=(shape, shape),...]
where the time goes in v5:
time: 58.9 us; the launch traced here: 58.7 us
  Pallas kernels  56.7 us (96%)
  local copies, waits for them, and re-layouts  1.41 us (2%)
  between operations  0.64 us (1%)
    pallas_call x1, Pallas kernels, local(): pl.pallas_call(functools.partial(kernel, dims), out_shape=(shape, shape),...  56.7 us
    unnamed x2, local copies, waits for them, and re-layouts  1.41 us

profile of v5, /device:TPU:0, one launch (start us, length us, event | category | flops | bytes accessed | tf_op | source)
XLA Modules:
  0.0 58.7 jit_solution(2907637612758957801)
XLA Ops:
  0.6 56.7 %shard_map.41 = (f32[16,32,128]{2,1,0:T(8,128)S(1)}, f32[16,32,128]{2,1,0:T(8,128)S(1)}) custom-call(f32[16,32,128]{2,1,0:T(8,128)} %x_hbm.1, f32[16,32,128]{2,1,0:T(8,128)} %d_hbm.1), custom_call_target="tpu_custom_call" | custom-call | tf_op jit(solution)/shard_map/pallas_call | solution.py:779
  57.3 0.7 %copy.6 = f32[16,32,128]{2,1,0:T(8,128)} copy(f32[16,32,128]{2,1,0:T(8,128)S(1)} %get-tuple-element.2) | data formatting | bytes 524288
  58.0 0.7 %copy.7 = f32[16,32,128]{2,1,0:T(8,128)} copy(f32[16,32,128]{2,1,0:T(8,128)S(1)} %get-tuple-element.3) | data formatting | bytes 524288

commit v6 on v5

--- a/solution.py
+++ b/solution.py
@@ -540,7 +540,7 @@
         def down0(p):
             return put(Z, p, (M0[...] * xin0(p)) * (R[p] * (k3 - k2 * D[p]) + k2 * box(R, p)))
 
-        loop(H - 1, H + nx + 1, down0, 6)
+        loop(H - 1, H + nx + 1, down0, 9)
 
         def rest0(p):
             return R[p] - ((27.0 + D[p]) * Z[p] - box(Z, p))
@@ -551,10 +551,9 @@
         def down1(p):
             return put_mid(R1a, p, 0.5 * M1[MID] * shrink0(p))
 
-        loop(H, H + n1x, pair0, 4)
+        loop(H, H + n1x, pair0, 8)
         loop(H, H + n1x, down1, 8)
 
-        pack1(it, R1a)
         fine1 = [level1(ex, it, 5)]
 
         Z1[H - 3 : H - 1] = none
@@ -576,6 +575,7 @@
         ring2 = jnp.where(lane // n2z % 2 == 0, low, high)
         tile[it, n2y : n2y + n2y // 2] = ring2[0 : n2y // 2]
         gather_start(1 + it)
+        pack1(it, R1a)
         start(fine1, FLAT + PACKED)
 
         far(it)
@@ -659,12 +659,12 @@
         def t0(p):
             return put(T, p, (M0[...] * xin0(p)) * rest0(p))
 
-        loop(H - 2, H + nx + 2, t0, 5)
+        loop(H - 2, H + nx + 2, t0, 10)
 
         def z0(p):
             return put(Z, p, Z[p] + (M0[...] * xin0(p)) * (T[p] * (k3 - k2 * D[p]) + k2 * box(T, p)))
 
-        loop(H - 1, H + nx + 1, z0, 6)
+        loop(H - 1, H + nx + 1, z0, 9)
 
     core = (slice(H, H + ny), slice(0, nz))
 

time: 58.9 us -> 58.7 us (level)
  no operation moved by 1% of the time
where the time goes in v6:
time: 58.7 us; the launch traced here: 58.6 us
  Pallas kernels  56.5 us (96%)
  local copies, waits for them, and re-layouts  1.41 us (2%)
  between operations  0.64 us (1%)
    pallas_call x1, Pallas kernels, local(): pl.pallas_call(functools.partial(kernel, dims), out_shape=(shape, shape),...  56.5 us
    unnamed x2, local copies, waits for them, and re-layouts  1.41 us

profile of v6, /device:TPU:0, one launch (start us, length us, event | category | flops | bytes accessed | tf_op | source)
XLA Modules:
  0.0 58.6 jit_solution(8887378261518629583)
XLA Ops:
  0.6 56.5 %shard_map.41 = (f32[16,32,128]{2,1,0:T(8,128)S(1)}, f32[16,32,128]{2,1,0:T(8,128)S(1)}) custom-call(f32[16,32,128]{2,1,0:T(8,128)} %x_hbm.1, f32[16,32,128]{2,1,0:T(8,128)} %d_hbm.1), custom_call_target="tpu_custom_call" | custom-call | tf_op jit(solution)/shard_map/pallas_call | solution.py:779
  57.1 0.7 %copy.6 = f32[16,32,128]{2,1,0:T(8,128)} copy(f32[16,32,128]{2,1,0:T(8,128)S(1)} %get-tuple-element.2) | data formatting | bytes 524288
  57.9 0.7 %copy.7 = f32[16,32,128]{2,1,0:T(8,128)} copy(f32[16,32,128]{2,1,0:T(8,128)S(1)} %get-tuple-element.3) | data formatting | bytes 524288
